TPU v7x, 32 devices: a whole 2x2x4 slice. The times are simulated.
32 devices in a mesh: freq: 8 (over z, x), pts: 4 (over y, core).
Axes of the slice: x: 2, y: 2, z: 4, core: 2. Of those that a mesh axis runs over, the one named last changes fastest.
Arguments:
- snapshots: float32 [256, 5, 8192], P(None, None, ('pts', 'freq')), may hold values from -6 to 6
- weights: float32 [8192], P(('pts', 'freq')), may hold values from 0.25 to 4
- starts: int32 [3], replicated, may hold values from 0 to 128
- bins: int32 [64], replicated, may hold values from 0 to 63, each once
Outputs:
- modes: float32 [64, 2, 5, 8192], P('freq', None, None, 'pts')
- energy: float32 [64], P('freq')
All inputs are finite; a program needn't handle non-finite values.
Results may differ from a plain program's by a relative error of at most 0.00024.
Values sent between devices are 32-bit elements; how exact they have to be, the bound alone decides.
A program may use at most 64 MiB of HBM per device.

v0:
```python
import functools
import math

import jax
import jax.numpy as jnp
import numpy as np
from jax import lax
from jax.experimental import pallas as pl
from jax.experimental.pallas import tpu as pltpu
from jax.sharding import PartitionSpec as P

NFFT = 128
ITERS = 8
LANES = 128
SUB = 8
MESH = pl.DeviceIdType.MESH


def base_table(nfft):
    steps = np.arange(nfft)
    window = 0.5 - 0.5 * np.cos(2.0 * math.pi * steps / nfft)
    scale = 1.0 / np.sqrt(np.sum(window * window))
    phase = (np.arange(nfft // 2)[:, None] * steps[None, :] % nfft) * (2.0 * math.pi / nfft)
    return np.concatenate([np.cos(phase) * scale, -np.sin(phase) * scale], 1).astype(np.float32)


def window_table(nfft, n_time):
    rel = np.arange(n_time)[None, :] - np.arange(n_time - nfft + 1)[:, None]
    window = 0.5 - 0.5 * np.cos(2.0 * math.pi * rel / nfft)
    return np.where((rel >= 0) & (rel < nfft), window, 0.0).astype(np.float32)


def split(x):
    hi = x.astype(jnp.bfloat16)
    lo = (x - hi.astype(jnp.float32)).astype(jnp.bfloat16)
    return hi, lo


def pick_rows(rows, shape):
    index = lax.broadcasted_iota(jnp.int32, shape, 0)
    out = jnp.zeros(shape, rows[0].dtype)
    for r, value in enumerate(rows):
        out = jnp.where(index == r, value, out)
    return out


def kernel(
    n_freq, n_pts, n_blocks, count, snap_hbm, w_hbm, starts_ref, bins_smem, bins_hbm, base_hbm, window_hbm,
    recv_ref, energy_ref,
    snap, w_ref, bins_ref, base_ref, window_ref, energy_out, tab, tab3, spec, gacc, gsend1, grecv1, gsend2, grecv2, coef, send, laid,
    load_sem, small_sem, s1, r1, s2, r2, s3, r3, own_sem,
):
    n_var, n_time, n_local = snap.shape
    n_bins = bins_smem.shape[0]
    per = n_bins // n_freq
    tiles = n_local // LANES
    step = n_var * tiles * 2
    fr = lax.axis_index("freq")
    pt = lax.axis_index("pts")

    small = [
        pltpu.make_async_copy(src, dst, small_sem.at[i])
        for i, (src, dst) in enumerate(
            [(base_hbm, base_ref), (window_hbm, window_ref), (w_hbm, w_ref), (bins_hbm, bins_ref)]
        )
    ]
    for copy in small:
        copy.start()
    for v in range(n_var):
        pltpu.make_async_copy(snap_hbm.at[v], snap.at[v], load_sem.at[v]).start()

    barrier = pltpu.get_barrier_semaphore()
    for d in range(1, n_pts):
        pl.semaphore_signal(barrier, inc=1, device_id={"pts": lax.rem(pt + d, n_pts)}, device_id_type=MESH)
    for d in range(1, n_freq):
        pl.semaphore_signal(barrier, inc=1, device_id={"freq": lax.rem(fr + d, n_freq)}, device_id_type=MESH)

    for copy in small:
        copy.wait()
    for j in range(n_bins):
        tab[pl.ds(j, 1), :] = base_ref[pl.ds(bins_smem[j], 1), :]
    starts = [starts_ref[b] for b in range(n_blocks)]
    cs = tab[:, :NFFT]
    sn = tab[:, NFFT:]
    reps = n_time // NFFT
    full = jnp.concatenate([jnp.concatenate([cs] * reps, 1), jnp.concatenate([sn] * reps, 1)], 0)
    for b in range(n_blocks):
        hi, lo = split(full * window_ref[pl.ds(starts[b], 1), :])
        rows = pl.ds(b * 2 * n_bins, 2 * n_bins)
        tab3[rows, 0:n_time] = hi
        tab3[rows, n_time : 2 * n_time] = lo
        tab3[rows, 2 * n_time : 3 * n_time] = hi

    wts = [jnp.broadcast_to(w_ref[:, l * LANES : (l + 1) * LANES], (SUB, LANES)) for l in range(tiles)]
    pairs = [(a, c) for a in range(n_blocks) for c in range(a + 1, n_blocks)]
    n_entries = n_blocks * n_blocks

    if n_entries % 2:
        gacc[n_entries * n_bins :, :] = jnp.zeros((n_bins, LANES), jnp.float32)
    for v in range(n_var):
        pltpu.make_async_copy(snap_hbm.at[v], snap.at[v], load_sem.at[v]).wait()
        x = snap[v]
        x = x - jnp.sum(x, 0, keepdims=True) * (1.0 / n_time)
        hi, lo = split(x)
        x3 = jnp.concatenate([hi, hi, lo], 0)
        spec[:, v * n_local : (v + 1) * n_local] = jnp.dot(
            tab3[...], x3, preferred_element_type=jnp.float32
        )
        for g in range(n_bins // SUB):
            total = [None] * n_entries
            for l in range(tiles):
                lane = slice((v * tiles + l) * LANES, (v * tiles + l + 1) * LANES)
                part = [
                    [spec[pl.ds((b * 2 + c) * n_bins + g * SUB, SUB), lane] for c in range(2)]
                    for b in range(n_blocks)
                ]
                wp = [[part[b][c] * wts[l] for c in range(2)] for b in range(n_blocks)]
                new = [wp[b][0] * part[b][0] + wp[b][1] * part[b][1] for b in range(n_blocks)]
                for a, c in pairs:
                    new.append(wp[a][0] * part[c][0] + wp[a][1] * part[c][1])
                    new.append(wp[a][0] * part[c][1] - wp[a][1] * part[c][0])
                total = [n if t is None else t + n for t, n in zip(total, new)]
            for e in range(n_entries):
                rows = pl.ds(e * n_bins + g * SUB, SUB)
                gacc[rows, :] = total[e] if v == 0 else gacc[rows, :] + total[e]

    ones = jnp.ones((SUB, 2 * LANES), jnp.bfloat16)
    rows = []
    for p in range((n_entries + 1) // 2):
        hi, lo = split(gacc[pl.ds(p * 2 * n_bins, 2 * n_bins), :])
        rows.append(
            lax.dot_general(
                ones, jnp.concatenate([hi, lo], 1), (((1,), (1,)), ((), ())),
                preferred_element_type=jnp.float32,
            )
        )
    mine = pick_rows(rows, (SUB, 2 * n_bins))[: len(rows)]
    gsend1[...] = mine
    grecv1[pt] = mine

    pl.semaphore_wait(barrier, n_pts + n_freq - 2)

    def exchange(axis, me, n, src, dst, send_sems, recv_sems, meanwhile=lambda: None):
        copies = []
        for d in range(1, n):
            copy = pltpu.make_async_remote_copy(
                src_ref=src, dst_ref=dst.at[me], send_sem=send_sems.at[d - 1], recv_sem=recv_sems.at[me],
                device_id={axis: lax.rem(me + d, n)}, device_id_type=MESH,
            )
            copy.start()
            copies.append(copy)
        done = meanwhile()
        for d in range(1, n):
            other = lax.rem(me + d, n)
            pltpu.make_async_remote_copy(
                src_ref=src, dst_ref=dst.at[other], send_sem=send_sems.at[d - 1], recv_sem=recv_sems.at[other],
                device_id={axis: other}, device_id_type=MESH,
            ).wait_recv()
        for copy in copies:
            copy.wait_send()
        total = [dst[i] for i in range(n)]
        while len(total) > 1:
            total = [sum(total[i + 1 : i + 2], total[i]) for i in range(0, len(total), 2)]
        return total[0], done

    def phases():
        both = jnp.concatenate([bins_ref[...], bins_ref[...]], 1)
        turn = (both * pick_rows(starts, (SUB, 2 * n_bins))) & (NFFT - 1)
        turn = jnp.where(turn >= NFFT // 2, turn - NFFT, turn)
        angle = turn.astype(jnp.float32) * (2.0 * math.pi / NFFT)
        return jnp.cos(angle), jnp.sin(angle)

    part, _ = exchange("pts", pt, n_pts, gsend1, grecv1, s1, r1)
    gsend2[...] = part
    grecv2[fr] = part
    gram, (ph_re, ph_im) = exchange("freq", fr, n_freq, gsend2, grecv2, s2, r2, phases)
    gram = gram * (1.0 / count)
    swapped = pltpu.roll(gram, n_bins, 1)
    entries = [(swapped if e % 2 else gram)[e // 2 : e // 2 + 1, :] for e in range(n_entries)]
    g_re = {(b, b): entries[b] for b in range(n_blocks)}
    g_im = {}
    for i, (a, c) in enumerate(pairs):
        g_re[a, c] = g_re[c, a] = entries[n_blocks + 2 * i]
        g_im[a, c] = entries[n_blocks + 2 * i + 1]
        g_im[c, a] = -g_im[a, c]

    def apply_gram(xr, xi):
        ur, ui = [], []
        for a in range(n_blocks):
            others = [c for c in range(n_blocks) if c != a]
            ur.append(
                sum([g_re[a, c] * xr[c] - g_im[a, c] * xi[c] for c in others], g_re[a, a] * xr[a])
            )
            ui.append(
                sum([g_re[a, c] * xi[c] + g_im[a, c] * xr[c] for c in others], g_re[a, a] * xi[a])
            )
        return ur, ui

    xr = [ph_re[b : b + 1, :] for b in range(n_blocks)]
    xi = [ph_im[b : b + 1, :] for b in range(n_blocks)]
    for _ in range(ITERS):
        ur, ui = apply_gram(xr, xi)
        squares = [r * r + i * i for r, i in zip(ur, ui)]
        inv = lax.rsqrt(sum(squares[1:], squares[0]))
        xr = [r * inv for r in ur]
        xi = [i * inv for i in ui]
    ur, ui = apply_gram(xr, xi)
    terms = [xr[b] * ur[b] + xi[b] * ui[b] for b in range(n_blocks)]
    energy = sum(terms[1:], terms[0])
    energy_out[...] = energy
    energy_copy = pltpu.make_async_copy(energy_out, energy_ref, small_sem.at[0])
    energy_copy.start()
    factor = lax.rsqrt(jnp.maximum(energy, 0.25))
    coef[...] = jnp.transpose(pick_rows([r * factor for r in xr + xi], (SUB, 2 * n_bins)))

    groups = n_bins // SUB
    per_group = SUB // per
    half = groups // 2
    my_group = fr // per_group
    order = [
        (1 - my_group // half) * half + lax.rem(lax.rem(my_group, half) + i, half) for i in range(half)
    ] + [(my_group // half) * half + lax.rem(lax.rem(my_group, half) + i, half) for i in range(1, half)]
    order.append(my_group)
    sent = []

    def ship(slot, place, dest):
        copy = pltpu.make_async_remote_copy(
            src_ref=laid.at[pl.ds(slot * SUB + place * per, per)],
            dst_ref=recv_ref.at[:, :, :, pl.ds(pl.multiple_of(fr * n_local, LANES), n_local)],
            send_sem=s3.at[len(sent)],
            recv_sem=r3.at[fr],
            device_id={"freq": dest},
            device_id_type=MESH,
        )
        copy.start()
        sent.append(copy)

    for slot, g in enumerate(order):
        first = pl.multiple_of(g * SUB, SUB)
        col = coef[pl.ds(first, SUB), :]
        cr = [jnp.broadcast_to(col[:, b : b + 1], (SUB, LANES)) for b in range(n_blocks)]
        ci = [
            jnp.broadcast_to(col[:, n_blocks + b : n_blocks + b + 1], (SUB, LANES)) for b in range(n_blocks)
        ]
        for j in range(n_var * tiles):
            lane = slice(j * LANES, (j + 1) * LANES)
            re = im = None
            for b in range(n_blocks):
                sr = spec[pl.ds(pl.multiple_of(b * 2 * n_bins + first, SUB), SUB), lane]
                si = spec[pl.ds(pl.multiple_of((b * 2 + 1) * n_bins + first, SUB), SUB), lane]
                tr = cr[b] * sr - ci[b] * si
                ti = cr[b] * si + ci[b] * sr
                re = tr if re is None else re + tr
                im = ti if im is None else im + ti
            send[pl.ds(slot * SUB * step + j * 2, SUB, stride=step), :] = re
            send[pl.ds(slot * SUB * step + j * 2 + 1, SUB, stride=step), :] = im
        for k in range(slot * SUB, (slot + 1) * SUB):
            for v in range(n_var):
                for l in range(tiles):
                    row = k * step + (v * tiles + l) * 2
                    laid[k, v, :, l * LANES : (l + 1) * LANES] = send[row : row + 2, :]
        if slot < groups - 1:
            for place in range(per_group):
                ship(slot, place, g * per_group + place)
        else:
            here = lax.rem(fr, per_group)
            for r in range(1, per_group):
                place = lax.rem(here + r, per_group)
                ship(slot, place, g * per_group + place)
            own = pltpu.make_async_copy(
                laid.at[pl.ds(slot * SUB + here * per, per)],
                recv_ref.at[:, :, :, pl.ds(pl.multiple_of(fr * n_local, LANES), n_local)],
                own_sem,
            )
            own.start()
    for copy in sent:
        copy.wait_send()
    own.wait()
    energy_copy.wait()
    for d in range(1, n_freq):
        other = lax.rem(fr + d, n_freq)
        pltpu.make_async_remote_copy(
            src_ref=laid.at[pl.ds(0, per)],
            dst_ref=recv_ref.at[:, :, :, pl.ds(pl.multiple_of(other * n_local, LANES), n_local)],
            send_sem=s3.at[0], recv_sem=r3.at[other], device_id={"freq": other}, device_id_type=MESH,
        ).wait_recv()


def place(n_freq, recv_hbm, energy_hbm, out_hbm, mine_hbm, got, energy, mine, in_sem, out_sem):
    per = got.shape[0]
    loads = [pltpu.make_async_copy(energy_hbm, energy, in_sem.at[per])]
    loads += [pltpu.make_async_copy(recv_hbm.at[k], got.at[k], in_sem.at[k]) for k in range(per)]
    for copy in loads:
        copy.start()
    fr = lax.axis_index("freq")
    loads[0].wait()
    chosen = jnp.zeros((1, per), jnp.float32)
    for f in range(n_freq):
        chosen = jnp.where(fr == f, energy[:, f * per : (f + 1) * per], chosen)
    mine[...] = chosen
    stores = [pltpu.make_async_copy(mine, mine_hbm, out_sem.at[per])]
    stores += [pltpu.make_async_copy(got.at[k], out_hbm.at[k], out_sem.at[k]) for k in range(per)]
    stores[0].start()
    for k in range(per):
        loads[k + 1].wait()
        stores[k + 1].start()
    for copy in stores:
        copy.wait()


def body(n_freq, n_pts, snapshots, weights, starts, bins):
    n_time, n_var, n_local = snapshots.shape
    n_blocks = starts.shape[0]
    n_bins = bins.shape[0]
    per = n_bins // n_freq
    tiles = n_local // LANES
    step = n_var * tiles * 2
    count = float(n_local * n_freq * n_pts * n_var)
    f32 = jnp.float32
    entries = n_blocks * n_blocks + (n_blocks * n_blocks) % 2
    vmem = pl.BlockSpec(memory_space=pltpu.VMEM)
    smem = pl.BlockSpec(memory_space=pltpu.SMEM)
    anyspace = pl.BlockSpec(memory_space=pl.ANY)
    dma = pltpu.SemaphoreType.DMA
    recv, energy = pl.pallas_call(
        functools.partial(kernel, n_freq, n_pts, n_blocks, count),
        out_shape=(
            jax.ShapeDtypeStruct((per, n_var, 2, n_freq * n_local), f32),
            jax.ShapeDtypeStruct((1, 2 * n_bins), f32),
        ),
        in_specs=[anyspace, anyspace, smem, smem, anyspace, anyspace, anyspace],
        out_specs=(anyspace, anyspace),
        scratch_shapes=[
            pltpu.VMEM((n_var, n_time, n_local), f32),
            pltpu.VMEM((1, n_local), f32),
            pltpu.VMEM((1, n_bins), jnp.int32),
            pltpu.VMEM((NFFT // 2, 2 * NFFT), f32),
            pltpu.VMEM((n_time - NFFT + 1, n_time), f32),
            pltpu.VMEM((1, 2 * n_bins), f32),
            pltpu.VMEM((n_bins, 2 * NFFT), f32),
            pltpu.VMEM((n_blocks * 2 * n_bins, 3 * n_time), jnp.bfloat16),
            pltpu.VMEM((n_blocks * 2 * n_bins, n_var * n_local), f32),
            pltpu.VMEM((entries * n_bins, LANES), f32),
            pltpu.VMEM((entries // 2, 2 * n_bins), f32),
            pltpu.VMEM((n_pts, entries // 2, 2 * n_bins), f32),
            pltpu.VMEM((entries // 2, 2 * n_bins), f32),
            pltpu.VMEM((n_freq, entries // 2, 2 * n_bins), f32),
            pltpu.VMEM((2 * n_bins, SUB), f32),
            pltpu.VMEM((n_bins * step, LANES), f32),
            pltpu.VMEM((n_bins, n_var, 2, n_local), f32),
            dma((n_var,)),
            dma((4,)),
            dma((n_pts,)),
            dma((n_pts,)),
            dma((n_freq,)),
            dma((n_freq,)),
            dma((n_freq,)),
            dma((n_freq,)),
            dma,
        ],
        compiler_params=pltpu.CompilerParams(collective_id=0, has_side_effects=True),
    )(
        jnp.transpose(snapshots, (1, 0, 2)), weights.reshape(1, n_local), starts, bins,
        bins.reshape(1, n_bins), jnp.asarray(base_table(NFFT)), jnp.asarray(window_table(NFFT, n_time)),
    )
    modes, mine = pl.pallas_call(
        functools.partial(place, n_freq),
        out_shape=(
            jax.ShapeDtypeStruct((per, n_var, 2, n_freq * n_local), f32),
            jax.ShapeDtypeStruct((1, per), f32),
        ),
        in_specs=[anyspace, anyspace],
        out_specs=(anyspace, anyspace),
        scratch_shapes=[
            pltpu.VMEM((per, n_var, 2, n_freq * n_local), f32),
            pltpu.VMEM((1, 2 * n_bins), f32),
            pltpu.VMEM((1, per), f32),
            dma((per + 1,)),
            dma((per + 1,)),
        ],
    )(recv, energy)
    return jnp.transpose(modes, (0, 2, 1, 3)), mine[0]


def solution(mesh):
    in_specs = (P(None, None, ("pts", "freq")), P(("pts", "freq")), P(), P())
    out_specs = (P("freq", None, None, "pts"), P("freq"))
    f = functools.partial(body, mesh.shape["freq"], mesh.shape["pts"])
    return jax.shard_map(f, mesh=mesh, in_specs=in_specs, out_specs=out_specs, check_vma=False)
```

profile of v0, /device:TPU:0, one launch (start us, length us, event | category | flops | bytes accessed | tf_op | source)
XLA Modules:
  0.0 34.3 jit_solution(12186869793139255697)
XLA Ops:
  0.6 31.5 %shard_map.77 = (f32[8,5,2,2048]{3,2,1,0:T(2,128)}, f32[1,128]{1,0:T(1,128)}) custom-call(f32[5,256,256]{2,1,0:T(8,128)} %bitcast.5, f32[1,256]{1,0:T(1,128)} %bitcast.7, s32[3]{0:T(128)} %starts_ref.1, s32[64]{0:T(128)} %bins_smem.1, s32[1,64]{1,0:T(1,128)} %bitcast.6, f32[64,256]{1,0:T(8,128)} %constant.4.clone.base_hbm, f32[129,256]{1,0:T(8,128)} %constant.5.clone.window_hbm), custom_call_target="tpu_custom_call" | custom-call | tf_op jit(solution)/shard_map/pallas_call | solution.py:325
  32.1 2.2 %shard_map.78 = (f32[8,5,2,2048]{3,2,1,0:T(2,128)}, f32[1,8]{1,0:T(1,128)}) custom-call(f32[8,5,2,2048]{3,2,1,0:T(2,128)} %get-tuple-element.6.recv_hbm, f32[1,128]{1,0:T(1,128)} %get-tuple-element.7.energy_hbm), custom_call_target="tpu_custom_call" | custom-call | tf_op jit(solution)/shard_map/pallas_call | solution.py:366
where the time goes:
time: 34.5 us; the launch traced here: 34.3 us
  Pallas kernels  33.6 us (97%)
  between operations  0.64 us (2%)
    pallas_call x1, Pallas kernels, body(): pl.pallas_call(functools.partial(kernel, n_freq, n_pts, n_blocks, count),...  31.5 us
    pallas_call x1, Pallas kernels, body(): pl.pallas_call(functools.partial(place, n_freq), out_shape=(jax.ShapeDtyp...  2.16 us

commit v1 on v0

--- a/solution.py
+++ b/solution.py
@@ -45,10 +45,10 @@
 
 
 def kernel(
-    n_freq, n_pts, n_blocks, count, snap_hbm, w_hbm, starts_ref, bins_smem, bins_hbm, base_hbm, window_hbm,
+    n_freq, n_pts, n_blocks, count, snap_hbm, w_hbm, starts_hbm, bins_1d, bins_hbm, base_hbm, window_hbm,
     recv_ref, energy_ref,
-    snap, w_ref, bins_ref, base_ref, window_ref, energy_out, tab, tab3, spec, gacc, gsend1, grecv1, gsend2, grecv2, coef, send, laid,
-    load_sem, small_sem, s1, r1, s2, r2, s3, r3, own_sem,
+    snap, w_ref, bins_ref, base_ref, window_ref, tab, tab3, spec, gacc, gsend1, grecv1, gsend2, grecv2, coef, send, laid,
+    starts_ref, bins_smem, load_sem, small_sem, s1, r1, s2, r2, s3, r3, own_sem,
 ):
     n_var, n_time, n_local = snap.shape
     n_bins = bins_smem.shape[0]
@@ -61,7 +61,10 @@
     small = [
         pltpu.make_async_copy(src, dst, small_sem.at[i])
         for i, (src, dst) in enumerate(
-            [(base_hbm, base_ref), (window_hbm, window_ref), (w_hbm, w_ref), (bins_hbm, bins_ref)]
+            [
+                (bins_1d, bins_smem), (starts_hbm, starts_ref), (base_hbm, base_ref), (window_hbm, window_ref),
+                (w_hbm, w_ref), (bins_hbm, bins_ref),
+            ]
         )
     ]
     for copy in small:
@@ -207,9 +210,10 @@
     ur, ui = apply_gram(xr, xi)
     terms = [xr[b] * ur[b] + xi[b] * ui[b] for b in range(n_blocks)]
     energy = sum(terms[1:], terms[0])
-    energy_out[...] = energy
-    energy_copy = pltpu.make_async_copy(energy_out, energy_ref, small_sem.at[0])
-    energy_copy.start()
+    chosen = jnp.zeros((1, per), jnp.float32)
+    for f in range(n_freq):
+        chosen = jnp.where(fr == f, energy[:, f * per : (f + 1) * per], chosen)
+    energy_ref[...] = chosen
     factor = lax.rsqrt(jnp.maximum(energy, 0.25))
     coef[...] = jnp.transpose(pick_rows([r * factor for r in xr + xi], (SUB, 2 * n_bins)))
 
@@ -276,7 +280,6 @@
     for copy in sent:
         copy.wait_send()
     own.wait()
-    energy_copy.wait()
     for d in range(1, n_freq):
         other = lax.rem(fr + d, n_freq)
         pltpu.make_async_remote_copy(
@@ -286,24 +289,12 @@
         ).wait_recv()
 
 
-def place(n_freq, recv_hbm, energy_hbm, out_hbm, mine_hbm, got, energy, mine, in_sem, out_sem):
-    per = got.shape[0]
-    loads = [pltpu.make_async_copy(energy_hbm, energy, in_sem.at[per])]
-    loads += [pltpu.make_async_copy(recv_hbm.at[k], got.at[k], in_sem.at[k]) for k in range(per)]
-    for copy in loads:
+def place(recv, energy, out_hbm, mine_hbm, out_sem):
+    per = recv.shape[0]
+    stores = [pltpu.make_async_copy(energy, mine_hbm, out_sem.at[per])]
+    stores += [pltpu.make_async_copy(recv.at[k], out_hbm.at[k], out_sem.at[k]) for k in range(per)]
+    for copy in stores:
         copy.start()
-    fr = lax.axis_index("freq")
-    loads[0].wait()
-    chosen = jnp.zeros((1, per), jnp.float32)
-    for f in range(n_freq):
-        chosen = jnp.where(fr == f, energy[:, f * per : (f + 1) * per], chosen)
-    mine[...] = chosen
-    stores = [pltpu.make_async_copy(mine, mine_hbm, out_sem.at[per])]
-    stores += [pltpu.make_async_copy(got.at[k], out_hbm.at[k], out_sem.at[k]) for k in range(per)]
-    stores[0].start()
-    for k in range(per):
-        loads[k + 1].wait()
-        stores[k + 1].start()
     for copy in stores:
         copy.wait()
 
@@ -319,24 +310,22 @@
     f32 = jnp.float32
     entries = n_blocks * n_blocks + (n_blocks * n_blocks) % 2
     vmem = pl.BlockSpec(memory_space=pltpu.VMEM)
-    smem = pl.BlockSpec(memory_space=pltpu.SMEM)
     anyspace = pl.BlockSpec(memory_space=pl.ANY)
     dma = pltpu.SemaphoreType.DMA
     recv, energy = pl.pallas_call(
         functools.partial(kernel, n_freq, n_pts, n_blocks, count),
         out_shape=(
-            jax.ShapeDtypeStruct((per, n_var, 2, n_freq * n_local), f32),
-            jax.ShapeDtypeStruct((1, 2 * n_bins), f32),
+            pltpu.VMEM((per, n_var, 2, n_freq * n_local), f32),
+            pltpu.VMEM((1, per), f32),
         ),
-        in_specs=[anyspace, anyspace, smem, smem, anyspace, anyspace, anyspace],
-        out_specs=(anyspace, anyspace),
+        in_specs=[anyspace] * 7,
+        out_specs=(vmem, vmem),
         scratch_shapes=[
             pltpu.VMEM((n_var, n_time, n_local), f32),
             pltpu.VMEM((1, n_local), f32),
             pltpu.VMEM((1, n_bins), jnp.int32),
             pltpu.VMEM((NFFT // 2, 2 * NFFT), f32),
             pltpu.VMEM((n_time - NFFT + 1, n_time), f32),
-            pltpu.VMEM((1, 2 * n_bins), f32),
             pltpu.VMEM((n_bins, 2 * NFFT), f32),
             pltpu.VMEM((n_blocks * 2 * n_bins, 3 * n_time), jnp.bfloat16),
             pltpu.VMEM((n_blocks * 2 * n_bins, n_var * n_local), f32),
@@ -348,8 +337,10 @@
             pltpu.VMEM((2 * n_bins, SUB), f32),
             pltpu.VMEM((n_bins * step, LANES), f32),
             pltpu.VMEM((n_bins, n_var, 2, n_local), f32),
+            pltpu.SMEM((n_blocks,), jnp.int32),
+            pltpu.SMEM((n_bins,), jnp.int32),
             dma((n_var,)),
-            dma((4,)),
+            dma((6,)),
             dma((n_pts,)),
             dma((n_pts,)),
             dma((n_freq,)),
@@ -364,21 +355,15 @@
         bins.reshape(1, n_bins), jnp.asarray(base_table(NFFT)), jnp.asarray(window_table(NFFT, n_time)),
     )
     modes, mine = pl.pallas_call(
-        functools.partial(place, n_freq),
+        place,
         out_shape=(
             jax.ShapeDtypeStruct((per, n_var, 2, n_freq * n_local), f32),
             jax.ShapeDtypeStruct((1, per), f32),
         ),
-        in_specs=[anyspace, anyspace],
+        in_specs=[vmem, vmem],
         out_specs=(anyspace, anyspace),
-        scratch_shapes=[
-            pltpu.VMEM((per, n_var, 2, n_freq * n_local), f32),
-            pltpu.VMEM((1, 2 * n_bins), f32),
-            pltpu.VMEM((1, per), f32),
-            dma((per + 1,)),
-            dma((per + 1,)),
-        ],
-    )(recv, energy)
+        scratch_shapes=[dma((per + 1,))],
+    )(pltpu.with_memory_space_constraint(recv, pltpu.VMEM), pltpu.with_memory_space_constraint(energy, pltpu.VMEM))
     return jnp.transpose(modes, (0, 2, 1, 3)), mine[0]
 
 

time: 34.5 us -> 32.7 us (0.948)
  Pallas kernels: 33.6 us -> 31.9 us
    pallas_call x1, Pallas kernels: 2.16 us -> 0.91 us  [body(): pl.pallas_call(place, out_shape=(jax.ShapeDtypeStruct((per, n_var, 2, n_f...]
    pallas_call x1, Pallas kernels: 31.5 us -> 31 us  [body(): pl.pallas_call(functools.partial(kernel, n_freq, n_pts, n_blocks, count),...]
where the time goes in v1:
time: 32.7 us; the launch traced here: 32.6 us
  Pallas kernels  31.9 us (98%)
  between operations  0.64 us (2%)
    pallas_call x1, Pallas kernels, body(): pl.pallas_call(functools.partial(kernel, n_freq, n_pts, n_blocks, count),...  31 us
    pallas_call x1, Pallas kernels, body(): pl.pallas_call(place, out_shape=(jax.ShapeDtypeStruct((per, n_var, 2, n_f...  0.91 us

profile of v1, /device:TPU:0, one launch (start us, length us, event | category | flops | bytes accessed | tf_op | source)
XLA Modules:
  0.0 32.6 jit_solution(10659683506547026612)
XLA Ops:
  0.6 31.0 %shard_map.77 = (f32[8,5,2,2048]{3,2,1,0:T(2,128)S(1)}, f32[1,8]{1,0:T(1,128)S(1)}) custom-call(f32[5,256,256]{2,1,0:T(8,128)} %bitcast.5, f32[1,256]{1,0:T(1,128)} %bitcast.7, s32[3]{0:T(128)} %starts_hbm.1, s32[64]{0:T(128)} %bins_1d.1, s32[1,64]{1,0:T(1,128)} %bitcast.6, f32[64,256]{1,0:T(8,128)} %constant.4.clone.base_hbm, ...), custom_call_target="tpu_custom_call" | custom-call | tf_op jit(solution)/shard_map/pallas_call | solution.py:315
  31.7 0.9 %shard_map.78 = (f32[8,5,2,2048]{3,2,1,0:T(2,128)}, f32[1,8]{1,0:T(1,128)}) custom-call(f32[8,5,2,2048]{3,2,1,0:T(2,128)S(1)} %get-tuple-element.6.recv, f32[1,8]{1,0:T(1,128)S(1)} %get-tuple-element.7.energy), custom_call_target="tpu_custom_call" | custom-call | tf_op jit(solution)/shard_map/pallas_call | solution.py:357
